TPU v7x, 128 devices: a whole 4x4x4 slice. The times are simulated.
128 devices in a mesh: gz: 128 (over x, y, z, core).
Axes of the slice: x: 4, y: 4, z: 4, core: 2. Of those that a mesh axis runs over, the one named last changes fastest.
Arguments:
- velocity: float32 [3, 512, 256, 512], P(None, 'gz'), may hold values from -0.3 to 0.3
- offsets: float32 [3, 65536], P(None, 'gz'), may hold values from 1.2 to 1.8
- bases: int32 [3, 65536], P(None, 'gz'), may hold values from 0 to 511, as said below
- targets: float32 [3, 65536], P(None, 'gz'), may hold values from 1 to 2
- stiffness: float32 [65536], P('gz'), may hold values from 10 to 100
- active_block_count: int32 [128], P('gz'), may hold values from 1 to 2, as said below
Outputs:
- velocity_out: float32 [3, 512, 256, 512], P(None, 'gz')
- offsets_out: float32 [3, 65536], P(None, 'gz')
Inputs may be any that keep to these rules, and one draw needn't show every extreme that they name: `bases`: rows are x, y, z. x lies in 0..511 and y in 0..255; the z of marker m lies in the slab of index m // 512, from (m // 512) * 4 to (m // 512) * 4 + 3. `active_block_count`: in every draw some slab uses all 2 blocks.
All inputs are finite; a program needn't handle non-finite values.
Results may differ from a plain program's by a relative error of at most 0.0015.
Values may be sent and summed in bfloat16 or wider, within the bound.
A program may use at most 192 MiB of HBM per device.

v0:
```python
import functools
import math

import jax
import jax.numpy as jnp
from jax import lax
from jax.experimental import pallas as pl
from jax.experimental.pallas import tpu as pltpu
from jax.sharding import PartitionSpec as P

AXIS = "gz"
BLK = 256
STEPS = 2
DT = 0.2
NU = 0.3
CZ = 4
NY = 256
NX = 512
M = 512
MESH = pl.DeviceIdType.MESH
BF = jnp.bfloat16
F32 = jnp.float32


def weights(offsets):
    angle = offsets * (0.5 * math.pi)
    c = 0.25 * jnp.cos(angle)
    s = 0.25 * jnp.sin(angle)
    return (0.25 + c, 0.25 + s, 0.25 - c, 0.25 - s)


def pick(delta, taps):
    out = jnp.where(delta == 3, taps[3], 0.0)
    for j in (2, 1, 0):
        out = jnp.where(delta == j, taps[j], out)
    return out


def kernel(
    vel, off_ref, bases_ref, targ_ref, stiff_ref, act_ref,
    vout, oout,
    state, low, edge, halo, xtab, ytab, lhs, gains, zrows, pack, near, ret, back, offs,
    in_sem, out_sem, send_sem, recv_sem, psend, precv, rsend, rrecv,
):
    me = lax.axis_index(AXIS)
    count = lax.axis_size(AXIS)
    right = lax.rem(me + 1, count)
    left = lax.rem(me + count - 1, count)

    loads = {}
    for p in (0, 3, 1, 2):
        loads[p] = pltpu.make_async_copy(vel.at[:, p], state.at[0, p], in_sem.at[p])
        loads[p].start()

    barrier = pltpu.get_barrier_semaphore()
    for neighbour in (left, right):
        pl.semaphore_signal(barrier, inc=1, device_id=(neighbour,), device_id_type=MESH)

    lane = lax.broadcasted_iota(jnp.int32, (1, M), 1)
    living = jnp.where(lane < act_ref[...] * BLK, 1.0, 0.0)
    strength = living * stiff_ref[...]
    level = bases_ref[2:3, :] - me * CZ
    offs[...] = off_ref[...]

    def prepare(slot):
        o = offs[...]
        w = weights(o)
        force = strength * (targ_ref[...] - o)
        for j in range(4):
            pack[slot, 6 + j : 7 + j, :] = w[j][0:1]
            pack[slot, 10 + j : 11 + j, :] = w[j][1:2]
        pack[slot, 0:3, :] = force
        pack[slot, 14:16, :] = bases_ref[0:2, :].astype(F32)
        for z in range(7):
            row = pick(z - level, [w[j][2:3] for j in range(4)])
            if z < CZ:
                zrows[z, 0:1, 0:M] = row
                gains[z, 0:3, 0:M] = force * row
            else:
                pack[slot, 3 + z - CZ : 4 + z - CZ, :] = row

    def receive(slot):
        zrows[CZ - 1, 0:1, M:] = jnp.zeros((1, M), F32)
        for z in range(3):
            row = near[slot, 3 + z : 4 + z, :]
            zrows[z, 0:1, M:] = row
            gains[z, 0:3, M:] = near[slot, 0:3, :] * row

    def tables(source, slot, side):
        lanes = pl.ds(side * M, M)

        def xrow(i, _):
            r = pl.multiple_of(i * 16, 16)
            where = lax.broadcasted_iota(jnp.int32, (16, M), 0) + r
            delta = (where - source[slot, 14:15, :].astype(jnp.int32)) & (NX - 1)
            taps = [source[slot, 6 + j : 7 + j, :] for j in range(4)]
            xtab[pl.ds(r, 16), lanes] = pick(delta, taps).astype(BF)
            return 0

        lax.fori_loop(0, NX // 16, xrow, 0)

        def yrow(i, _):
            r = pl.multiple_of(i * 16, 16)
            where = lax.broadcasted_iota(jnp.int32, (16, M), 0) + r
            delta = (where - source[slot, 15:16, :].astype(jnp.int32)) & (NY - 1)
            taps = [source[slot, 10 + j : 11 + j, :] for j in range(4)]
            ytab[pl.ds(r, 16), lanes] = pick(delta, taps)
            return 0

        lax.fori_loop(0, NY // 16, yrow, 0)

    def spread(z, width, dst):
        def rows(i, _):
            r = pl.multiple_of(i * 16, 16)
            y = ytab[pl.ds(r, 16), 0:width]
            for c in range(3):
                lhs[pl.ds(c * NY + r, 16), 0:width] = (gains[z, c : c + 1, 0:width] * y).astype(BF)
            return 0

        lax.fori_loop(0, NY // 16, rows, 0)
        out = lax.dot_general(
            lhs[:, 0:width],
            xtab[:, 0:width],
            (((1,), (1,)), ((), ())),
            preferred_element_type=F32,
        )
        state[dst, z] = out.reshape(3, NY, NX)

    def spread_all(dst):
        def body(z, _):
            spread(z, 2 * M, dst)
            return 0

        lax.fori_loop(0, CZ - 1, body, 0)
        spread(CZ - 1, M, dst)

    def advance(p, src, dst, below, above):
        def rows(i, _):
            r = pl.multiple_of(i * 16, 16)
            rp = pl.multiple_of(lax.rem(r + NY - 8, NY), 8)
            rn = pl.multiple_of(lax.rem(r + 16, NY), 8)
            here = pl.ds(r, 16)
            v = [state[src, p, c, here, :] for c in range(3)]
            lower, upper = [], []
            for d in (2, 1, 0):
                scaled = (0.5 * DT) * v[d]
                upper.append(DT * NU - scaled)
                lower.append(DT * NU + scaled)
            for c in range(3):
                prev = state[src, p, c, pl.ds(rp, 8), :]
                nxt = state[src, p, c, pl.ds(rn, 8), :]
                total = DT * state[dst, p, c, here, :] + (1.0 - 6.0 * DT * NU) * v[c]
                total = total + upper[0] * above(c, here) + lower[0] * below(c, here)
                yup = pltpu.roll(jnp.concatenate([v[c], nxt], axis=0), 23, 0)[0:16]
                ydown = pltpu.roll(jnp.concatenate([prev, v[c]], axis=0), 1, 0)[8:24]
                total = total + upper[1] * yup + lower[1] * ydown
                total = total + upper[2] * pltpu.roll(v[c], NX - 1, 1) + lower[2] * pltpu.roll(v[c], 1, 1)
                state[dst, p, c, here, :] = total
                low[p, c, here, :] = total.astype(BF)
            return 0

        lax.fori_loop(0, NY // 16, rows, 0)

    def inner(src, plane):
        return lambda c, rows: state[src, plane, c, rows, :]

    def outer(step, side):
        return lambda c, rows: halo[step, side, c, rows, :].astype(F32)

    def sample(z, lanes):
        out = jnp.dot(low[z].reshape(3 * NY, NX), xtab[:, lanes], preferred_element_type=F32)
        y = ytab[:, lanes]
        parts = [jnp.sum(out[c * NY : (c + 1) * NY] * y, axis=0, keepdims=True) for c in range(3)]
        return jnp.concatenate(parts, axis=0) * zrows[z, 0:1, lanes]

    own = slice(0, M)
    other = slice(M, 2 * M)

    waits = []
    for step in range(STEPS):
        src, dst = step % 2, (step + 1) % 2
        prepare(step)
        if step == 0:
            for side, p in ((0, 0), (1, 3)):
                loads[p].wait()

                def lower_rows(i, _, side=side, p=p):
                    r = pl.multiple_of(i * 16, 16)
                    for c in range(3):
                        edge[side, c, pl.ds(r, 16), :] = state[0, p, c, pl.ds(r, 16), :].astype(BF)
                    return 0

                lax.fori_loop(0, NY // 16, lower_rows, 0)
            pl.semaphore_wait(barrier, 2)
        packet = pltpu.make_async_remote_copy(
            src_ref=pack.at[step], dst_ref=near.at[step],
            send_sem=psend.at[step], recv_sem=precv.at[step],
            device_id=(right,), device_id_type=MESH,
        )
        packet.start()
        if step == 0:
            copies = []
            for side, target in ((0, left), (1, right)):
                copies.append(pltpu.make_async_remote_copy(
                    src_ref=edge.at[side], dst_ref=halo.at[0, 1 - side],
                    send_sem=send_sem.at[0, side], recv_sem=recv_sem.at[0, 1 - side],
                    device_id=(target,), device_id_type=MESH,
                ))
                copies[-1].start()
        tables(pack, step, 0)
        packet.wait_recv()
        receive(step)
        tables(near, step, 1)
        spread_all(dst)
        if step == 0:
            loads[1].wait()
            loads[2].wait()
        for c in copies:
            c.wait_recv()
            c.wait_send()
        advance(0, src, dst, outer(step, 0), inner(src, 1))
        advance(3, src, dst, inner(src, 2), outer(step, 1))
        if step + 1 < STEPS:
            copies = []
            for side, plane, target in ((0, 0, left), (1, 3, right)):
                copies.append(pltpu.make_async_remote_copy(
                    src_ref=low.at[plane], dst_ref=halo.at[step + 1, 1 - side],
                    send_sem=send_sem.at[step + 1, side], recv_sem=recv_sem.at[step + 1, 1 - side],
                    device_id=(target,), device_id_type=MESH,
                ))
        advance(1, src, dst, inner(src, 0), inner(src, 2))
        if step + 1 < STEPS:
            for c in copies:
                c.start()
        advance(2, src, dst, inner(src, 1), inner(src, 3))
        if step + 1 == STEPS:
            stores = [pltpu.make_async_copy(state.at[dst, p], vout.at[:, p], out_sem.at[p]) for p in range(CZ)]
            for c in stores:
                c.start()

        def near_sample(z, acc):
            return acc + sample(z, other)

        ret[step, 0:3, :] = lax.fori_loop(0, CZ - 1, near_sample, jnp.zeros((3, M), F32))
        acc = sample(0, own)
        answer = pltpu.make_async_remote_copy(
            src_ref=ret.at[step], dst_ref=back.at[step],
            send_sem=rsend.at[step], recv_sem=rrecv.at[step],
            device_id=(left,), device_id_type=MESH,
        )
        answer.start()
        acc = lax.fori_loop(1, CZ, lambda z, a: a + sample(z, own), acc)
        answer.wait_recv()
        offs[...] = offs[...] + DT * (living * (acc + back[step, 0:3, :]))
        waits += [packet, answer]
    oout[...] = offs[...]
    for c in waits:
        c.wait_send()
    for c in stores:
        c.wait()


def local(velocity, offsets, bases, targets, stiffness, active_block_count):
    vmem = pl.BlockSpec(memory_space=pltpu.VMEM)
    hbm = pl.BlockSpec(memory_space=pl.ANY)
    return pl.pallas_call(
        kernel,
        out_shape=(
            jax.ShapeDtypeStruct(velocity.shape, F32),
            jax.ShapeDtypeStruct(offsets.shape, F32),
        ),
        in_specs=[hbm, vmem, vmem, vmem, vmem, vmem],
        out_specs=(hbm, vmem),
        scratch_shapes=[
            pltpu.VMEM((2, CZ, 3, NY, NX), F32),
            pltpu.VMEM((CZ, 3, NY, NX), BF),
            pltpu.VMEM((2, 3, NY, NX), BF),
            pltpu.VMEM((STEPS, 2, 3, NY, NX), BF),
            pltpu.VMEM((NX, 2 * M), BF),
            pltpu.VMEM((NY, 2 * M), F32),
            pltpu.VMEM((3 * NY, 2 * M), BF),
            pltpu.VMEM((CZ, 8, 2 * M), F32),
            pltpu.VMEM((CZ, 8, 2 * M), F32),
            pltpu.VMEM((STEPS, 16, M), F32),
            pltpu.VMEM((STEPS, 16, M), F32),
            pltpu.VMEM((STEPS, 8, M), F32),
            pltpu.VMEM((STEPS, 8, M), F32),
            pltpu.VMEM((3, M), F32),
            pltpu.SemaphoreType.DMA((CZ,)),
            pltpu.SemaphoreType.DMA((CZ,)),
            pltpu.SemaphoreType.DMA((STEPS, 2)),
            pltpu.SemaphoreType.DMA((STEPS, 2)),
            pltpu.SemaphoreType.DMA((STEPS,)),
            pltpu.SemaphoreType.DMA((STEPS,)),
            pltpu.SemaphoreType.DMA((STEPS,)),
            pltpu.SemaphoreType.DMA((STEPS,)),
        ],
        compiler_params=pltpu.CompilerParams(
            collective_id=0, has_side_effects=True, vmem_limit_bytes=60 * 1024 * 1024
        ),
    )(
        velocity,
        offsets,
        bases,
        targets,
        stiffness.reshape(1, -1),
        active_block_count.reshape(1, 1),
    )


def solution(mesh):
    return jax.shard_map(
        local,
        mesh=mesh,
        in_specs=(
            P(None, AXIS, None, None),
            P(None, AXIS),
            P(None, AXIS),
            P(None, AXIS),
            P(AXIS),
            P(AXIS),
        ),
        out_specs=(P(None, AXIS, None, None), P(None, AXIS)),
        check_vma=False,
    )
```

profile of v0, /device:TPU:0, one launch (start us, length us, event | category | flops | bytes accessed | tf_op | source)
XLA Modules:
  0.0 72.2 jit_solution(13457928763918541388)
XLA Ops:
  1.3 64.1 %shard_map.77 = (f32[3,4,256,512]{3,2,1,0:T(8,128)}, f32[3,512]{1,0:T(4,128)}) custom-call(f32[3,4,256,512]{3,2,1,0:T(8,128)} %vel.1, f32[3,512]{1,0:T(4,128)} %off_ref.1, s32[3,512]{1,0:T(4,128)} %bases_ref.1, f32[3,512]{1,0:T(4,128)} %targ_ref.1, f32[1,512]{1,0:T(1,128)} %bitcast.3, s32[1,1]{1,0:T(1,128)} %bitcast.2.act_ref), custom_call_target="tpu_custom_call" | custom-call | tf_op jit(solution)/shard_map/pallas_call | solution.py:266
  65.4 0.0 copy-start
  65.4 6.2 %copy.11 = f32[3,4,256,512]{3,2,1,0:T(8,128)} copy(f32[3,4,256,512]{3,2,1,0:T(8,128)} %get-tuple-element.4) | data formatting | bytes 12582912
  71.6 0.0 copy-done
  71.6 0.6 copy.12
Async XLA Ops:
  65.4 6.2 %copy-start = (f32[3,512]{1,0:T(4,128)S(1)}, f32[3,512]{1,0:T(4,128)}, u32[]{:S(2)}) copy-start(f32[3,512]{1,0:T(4,128)} %get-tuple-element.5) | copy-start | bytes 18436
where the time goes:
time: 72.4 us; the launch traced here: 72.2 us
  Pallas kernels  64.1 us (89%)
  local copies, waits for them, and re-layouts  6.8 us (9%)
  between operations  1.29 us (2%)
    pallas_call x1, Pallas kernels, local(): pl.pallas_call(kernel, out_shape=(jax.ShapeDtypeStruct(velocity.shape, F3...  64.1 us
    unnamed x4, local copies, waits for them, and re-layouts  6.8 us

commit v1 on v0

v1 whole, which is shorter than its diff:
```python
import functools
import math

import jax
import jax.numpy as jnp
from jax import lax
from jax.experimental import pallas as pl
from jax.experimental.pallas import tpu as pltpu
from jax.sharding import PartitionSpec as P

AXIS = "gz"
BLK = 256
STEPS = 2
DT = 0.2
NU = 0.3
CZ = 4
NY = 256
NX = 512
M = 512
MESH = pl.DeviceIdType.MESH
BF = jnp.bfloat16
F32 = jnp.float32


def weights(offsets):
    angle = offsets * (0.5 * math.pi)
    c = 0.25 * jnp.cos(angle)
    s = 0.25 * jnp.sin(angle)
    return (0.25 + c, 0.25 + s, 0.25 - c, 0.25 - s)


def pick(delta, taps):
    out = jnp.where(delta == 3, taps[3], 0.0)
    for j in (2, 1, 0):
        out = jnp.where(delta == j, taps[j], out)
    return out


def kernel(
    vel, off_in, bases_in, targ_in, stiff_in, act_in,
    vout, oout,
    spare, low, edge, halo, xtab, ytab, lhs, gains, zrows, pack, near, ret, back, offs, off_ref, bases_ref, targ_ref, stiff_ref, act_ref,
    in_sem, small_sem, send_sem, recv_sem, psend, precv, rsend, rrecv,
):
    state = (vout, spare)
    me = lax.axis_index(AXIS)
    count = lax.axis_size(AXIS)
    right = lax.rem(me + 1, count)
    left = lax.rem(me + count - 1, count)

    smalls = [
        pltpu.make_async_copy(a, b, small_sem.at[i])
        for i, (a, b) in enumerate((
            (off_in, off_ref), (bases_in, bases_ref), (targ_in, targ_ref),
            (stiff_in, stiff_ref), (act_in, act_ref),
        ))
    ]
    for copy in smalls:
        copy.start()
    loads = {}
    for p in (0, 3, 1, 2):
        loads[p] = pltpu.make_async_copy(vel.at[:, p], vout.at[:, p], in_sem.at[p])
        loads[p].start()

    barrier = pltpu.get_barrier_semaphore()
    for neighbour in (left, right):
        pl.semaphore_signal(barrier, inc=1, device_id=(neighbour,), device_id_type=MESH)

    for copy in smalls:
        copy.wait()
    lane = lax.broadcasted_iota(jnp.int32, (1, M), 1)
    living = jnp.where(lane < act_ref[...] * BLK, 1.0, 0.0)
    strength = living * stiff_ref[...]
    level = bases_ref[2:3, :] - me * CZ
    offs[...] = off_ref[...]

    def prepare(slot):
        o = offs[...]
        w = weights(o)
        force = strength * (targ_ref[...] - o)
        for j in range(4):
            pack[slot, 6 + j : 7 + j, :] = w[j][0:1]
            pack[slot, 10 + j : 11 + j, :] = w[j][1:2]
        pack[slot, 0:3, :] = force
        pack[slot, 14:16, :] = bases_ref[0:2, :].astype(F32)
        for z in range(7):
            row = pick(z - level, [w[j][2:3] for j in range(4)])
            if z < CZ:
                zrows[z, 0:1, 0:M] = row
                gains[z, 0:3, 0:M] = force * row
            else:
                pack[slot, 3 + z - CZ : 4 + z - CZ, :] = row

    def receive(slot):
        zrows[CZ - 1, 0:1, M:] = jnp.zeros((1, M), F32)
        gains[CZ - 1, 0:3, M:] = jnp.zeros((3, M), F32)
        for z in range(3):
            row = near[slot, 3 + z : 4 + z, :]
            zrows[z, 0:1, M:] = row
            gains[z, 0:3, M:] = near[slot, 0:3, :] * row

    def tables(source, slot, side):
        lanes = pl.ds(side * M, M)

        def xrow(i, _):
            r = pl.multiple_of(i * 16, 16)
            where = lax.broadcasted_iota(jnp.int32, (16, M), 0) + r
            delta = (where - source[slot, 14:15, :].astype(jnp.int32)) & (NX - 1)
            taps = [source[slot, 6 + j : 7 + j, :] for j in range(4)]
            xtab[pl.ds(r, 16), lanes] = pick(delta, taps).astype(BF)
            return 0

        lax.fori_loop(0, NX // 16, xrow, 0)

        def yrow(i, _):
            r = pl.multiple_of(i * 16, 16)
            where = lax.broadcasted_iota(jnp.int32, (16, M), 0) + r
            delta = (where - source[slot, 15:16, :].astype(jnp.int32)) & (NY - 1)
            taps = [source[slot, 10 + j : 11 + j, :] for j in range(4)]
            ytab[pl.ds(r, 16), lanes] = pick(delta, taps)
            return 0

        lax.fori_loop(0, NY // 16, yrow, 0)

    core = lax.rem(me, 2)
    partner = (me + 1 - 2 * core, lax.rem(me + count - 1 + 2 * core, count))
    plane = (3 - 3 * core, 3 * core)
    inside = (2 - core, 1 + core)
    side = 1.0 - 2.0 * core.astype(F32)
    sides = (side, -side)

    def stencil(p, src, dst, near_planes, sign=None):
        def rows(i, _):
            r = pl.multiple_of(i * 16, 16)
            rp = pl.multiple_of(lax.rem(r + NY - 8, NY), 8)
            rn = pl.multiple_of(lax.rem(r + 16, NY), 8)
            adjacent = [near_planes(c, pl.ds(r, 16)) for c in range(3)]
            tiles = [
                [src[c, p, pl.ds(rp, 8), :], src[c, p, pl.ds(r, 8), :],
                 src[c, p, pl.ds(r + 8, 8), :], src[c, p, pl.ds(rn, 8), :]]
                for c in range(3)
            ]
            for h in (0, 1):
                upper, lower = [], []
                for d in (2, 1, 0):
                    scaled = (0.5 * DT) * tiles[d][1 + h]
                    if d == 2 and sign is not None:
                        scaled = sign * scaled
                    upper.append(DT * NU - scaled)
                    lower.append(DT * NU + scaled)
                for c in range(3):
                    prev, v, nxt = tiles[c][h], tiles[c][h + 1], tiles[c][h + 2]
                    above, below = (x[8 * h : 8 * h + 8] for x in adjacent[c])
                    yup = pltpu.roll(jnp.concatenate([v, nxt], axis=0), 15, 0)[0:8]
                    ydown = pltpu.roll(jnp.concatenate([prev, v], axis=0), 1, 0)[8:16]
                    total = (1.0 - 6.0 * DT * NU) * v
                    total = total + upper[0] * above + lower[0] * below
                    total = total + upper[1] * yup + lower[1] * ydown
                    total = total + upper[2] * pltpu.roll(v, NX - 1, 1) + lower[2] * pltpu.roll(v, 1, 1)
                    dst[c, p, pl.ds(r + 8 * h, 8), :] = total
            return 0

        lax.fori_loop(0, NY // 16, rows, 0)

    def interior(src, dst):
        for p in (1, 2):
            stencil(p, src, dst, lambda c, rows: (src[c, p + 1, rows, :], src[c, p - 1, rows, :]))

    def border(k, step, src, dst):
        stencil(
            plane[k], src, dst,
            lambda c, rows: (halo[step, k, c, rows, :].astype(F32), src[c, inside[k], rows, :]),
            sides[k],
        )

    def spread(z, dst):
        for c in range(3):
            lhs[c * NY : (c + 1) * NY, :] = (gains[z, c : c + 1, :] * ytab[...]).astype(BF)
        out = lax.dot_general(
            lhs[...], xtab[...], (((1,), (1,)), ((), ())), preferred_element_type=F32
        )
        total = dst[:, z] + DT * out.reshape(3, NY, NX)
        dst[:, z] = total
        low[z] = total.astype(BF)

    def sample(z, lanes):
        out = jnp.dot(low[z].reshape(3 * NY, NX), xtab[:, lanes], preferred_element_type=F32)
        y = ytab[:, lanes]
        parts = [jnp.sum(out[c * NY : (c + 1) * NY] * y, axis=0, keepdims=True) for c in range(3)]
        return jnp.concatenate(parts, axis=0) * zrows[z, 0:1, lanes]

    own = slice(0, M)
    other = slice(M, 2 * M)

    def sending(step, k, ref):
        return pltpu.make_async_remote_copy(
            src_ref=ref, dst_ref=halo.at[step, k],
            send_sem=send_sem.at[step, k], recv_sem=recv_sem.at[step, k],
            device_id=(partner[k],), device_id_type=MESH,
        )

    waits = []
    for step in range(STEPS):
        src, dst = state[step % 2], state[(step + 1) % 2]
        prepare(step)
        if step == 0:
            loads[0].wait()
            loads[3].wait()
            for k in (1, 0):

                def lower_rows(i, _, k=k):
                    r = pl.multiple_of(i * 16, 16)
                    for c in range(3):
                        edge[k, c, pl.ds(r, 16), :] = vout[c, plane[k], pl.ds(r, 16), :].astype(BF)
                    return 0

                lax.fori_loop(0, NY // 16, lower_rows, 0)
            pl.semaphore_wait(barrier, 2)
        packet = pltpu.make_async_remote_copy(
            src_ref=pack.at[step], dst_ref=near.at[step],
            send_sem=psend.at[step], recv_sem=precv.at[step],
            device_id=(right,), device_id_type=MESH,
        )
        packet.start()
        if step == 0:
            copies = [sending(0, k, edge.at[k]) for k in range(2)]
            copies[1].start()
            copies[0].start()
        tables(pack, step, 0)
        if step == 0:
            loads[1].wait()
            loads[2].wait()
            interior(src, dst)
        copies[0].wait()
        border(0, step, src, dst)
        packet.wait_recv()
        receive(step)
        tables(near, step, 1)

        def two(z, _):
            spread(z, dst)
            return 0

        lax.fori_loop(1, 3, two, 0)
        spread(plane[0], dst)
        if step + 1 < STEPS:
            after = [sending(step + 1, k, low.at[plane[k]]) for k in range(2)]
        copies[1].wait()
        border(1, step, src, dst)
        spread(plane[1], dst)
        if step + 1 < STEPS:
            after[1].start()
            after[0].start()
            copies = after

        def near_sample(z, acc):
            return acc + sample(z, other)

        ret[step, 0:3, :] = lax.fori_loop(0, CZ - 1, near_sample, jnp.zeros((3, M), F32))
        acc = sample(0, own)
        answer = pltpu.make_async_remote_copy(
            src_ref=ret.at[step], dst_ref=back.at[step],
            send_sem=rsend.at[step], recv_sem=rrecv.at[step],
            device_id=(left,), device_id_type=MESH,
        )
        answer.start()
        acc = lax.fori_loop(1, CZ, lambda z, a: a + sample(z, own), acc)
        if step + 1 < STEPS:
            interior(dst, src)
        answer.wait_recv()
        offs[...] = offs[...] + DT * (living * (acc + back[step, 0:3, :]))
        waits += [packet, answer]
    oout[...] = offs[...]
    for c in waits:
        c.wait_send()


def local(velocity, offsets, bases, targets, stiffness, active_block_count):
    vmem = pl.BlockSpec(memory_space=pltpu.VMEM)
    hbm = pl.BlockSpec(memory_space=pltpu.HBM)
    return pl.pallas_call(
        kernel,
        out_shape=(
            jax.ShapeDtypeStruct(velocity.shape, F32),
            jax.ShapeDtypeStruct(offsets.shape, F32),
        ),
        in_specs=[hbm] * 6,
        out_specs=(vmem, vmem),
        scratch_shapes=[
            pltpu.VMEM((3, CZ, NY, NX), F32),
            pltpu.VMEM((CZ, 3, NY, NX), BF),
            pltpu.VMEM((2, 3, NY, NX), BF),
            pltpu.VMEM((STEPS, 2, 3, NY, NX), BF),
            pltpu.VMEM((NX, 2 * M), BF),
            pltpu.VMEM((NY, 2 * M), F32),
            pltpu.VMEM((3 * NY, 2 * M), BF),
            pltpu.VMEM((CZ, 8, 2 * M), F32),
            pltpu.VMEM((CZ, 8, 2 * M), F32),
            pltpu.VMEM((STEPS, 16, M), F32),
            pltpu.VMEM((STEPS, 16, M), F32),
            pltpu.VMEM((STEPS, 8, M), F32),
            pltpu.VMEM((STEPS, 8, M), F32),
            pltpu.VMEM((3, M), F32),
            pltpu.VMEM((3, M), F32),
            pltpu.VMEM((3, M), jnp.int32),
            pltpu.VMEM((3, M), F32),
            pltpu.VMEM((1, M), F32),
            pltpu.VMEM((1, 1), jnp.int32),
            pltpu.SemaphoreType.DMA((CZ,)),
            pltpu.SemaphoreType.DMA((5,)),
            pltpu.SemaphoreType.DMA((STEPS, 2)),
            pltpu.SemaphoreType.DMA((STEPS, 2)),
            pltpu.SemaphoreType.DMA((STEPS,)),
            pltpu.SemaphoreType.DMA((STEPS,)),
            pltpu.SemaphoreType.DMA((STEPS,)),
            pltpu.SemaphoreType.DMA((STEPS,)),
        ],
        compiler_params=pltpu.CompilerParams(
            collective_id=0, has_side_effects=True, vmem_limit_bytes=40 * 1024 * 1024
        ),
    )(*(
        pltpu.with_memory_space_constraint(a, pltpu.HBM)
        for a in (
            velocity,
            offsets,
            bases,
            targets,
            stiffness.reshape(1, -1),
        )
    ), active_block_count.reshape(1, 1))


def solution(mesh):
    return jax.shard_map(
        local,
        mesh=mesh,
        in_specs=(
            P(None, AXIS, None, None),
            P(None, AXIS),
            P(None, AXIS),
            P(None, AXIS),
            P(AXIS),
            P(AXIS),
        ),
        out_specs=(P(None, AXIS, None, None), P(None, AXIS)),
        check_vma=False,
    )
```

time: 72.4 us -> 58.1 us (0.80)
  Pallas kernels: 64.1 us -> 53.4 us
  local copies, waits for them, and re-layouts: 6.8 us -> 3.3 us
    pallas_call x1, Pallas kernels: 64.1 us -> 53.4 us  [local(): pl.pallas_call(kernel, out_shape=(jax.ShapeDtypeStruct(velocity.shape, F3...]
    unnamed x4 -> x2, local copies, waits for them, and re-layouts: 6.8 us -> 3.3 us
where the time goes in v1:
time: 58.1 us; the launch traced here: 58 us
  Pallas kernels  53.4 us (92%)
  local copies, waits for them, and re-layouts  3.3 us (6%)
  between operations  1.29 us (2%)
    pallas_call x1, Pallas kernels, local(): pl.pallas_call(kernel, out_shape=(jax.ShapeDtypeStruct(velocity.shape, F3...  53.4 us
    unnamed x2, local copies, waits for them, and re-layouts  3.3 us

profile of v1, /device:TPU:0, one launch (start us, length us, event | category | flops | bytes accessed | tf_op | source)
XLA Modules:
  0.0 58.0 jit_solution(16602820262062659546)
XLA Ops:
  1.3 53.4 %shard_map.77 = (f32[3,4,256,512]{3,2,1,0:T(8,128)S(1)}, f32[3,512]{1,0:T(4,128)S(1)}) custom-call(f32[3,4,256,512]{3,2,1,0:T(8,128)} %vel.1, f32[3,512]{1,0:T(4,128)} %off_in.1, s32[3,512]{1,0:T(4,128)} %bases_in.1, f32[3,512]{1,0:T(4,128)} %targ_in.1, f32[1,512]{1,0:T(1,128)} %bitcast.3, s32[1,1]{1,0:T(1,128)} %bitcast.2.act_in), custom_call_target="tpu_custom_call" | custom-call | tf_op jit(solution)/shard_map/pallas_call | solution.py:281
  54.7 2.7 %copy.11 = f32[3,4,256,512]{3,2,1,0:T(8,128)} copy(f32[3,4,256,512]{3,2,1,0:T(8,128)S(1)} %get-tuple-element.4) | data formatting | bytes 12582912
  57.4 0.6 %copy.12 = f32[3,512]{1,0:T(4,128)} copy(f32[3,512]{1,0:T(4,128)S(1)} %get-tuple-element.5) | data formatting | bytes 12288

commit v2 on v1

v2 whole, which is shorter than its diff:
```python
import math

import jax
import jax.numpy as jnp
from jax import lax
from jax.experimental import pallas as pl
from jax.experimental.pallas import tpu as pltpu
from jax.sharding import PartitionSpec as P

AXIS = "gz"
BLK = 256
STEPS = 2
DT = 0.2
NU = 0.3
CZ = 4
NY = 256
NX = 512
M = 512
LB = NX // 128
MESH = pl.DeviceIdType.MESH
BF = jnp.bfloat16
F32 = jnp.float32


def weights(offsets):
    angle = offsets * (0.5 * math.pi)
    c = 0.25 * jnp.cos(angle)
    s = 0.25 * jnp.sin(angle)
    return (0.25 + c, 0.25 + s, 0.25 - c, 0.25 - s)


def pick(delta, taps):
    out = jnp.where(delta == 3, taps[3], 0.0)
    for j in (2, 1, 0):
        out = jnp.where(delta == j, taps[j], out)
    return out


def kernel(
    vel, off_in, bases_in, targ_in, stiff_in, act_in,
    vout, oout,
    first, second, low, edge, halo, xtab, ytab, lhs, gains, zrows, taps, cells, marks, pack, near,
    part, got, offs, bases_ref, targ_ref, stiff_ref, act_ref,
    in_sem, small_sem, send_sem, recv_sem, psend, precv, rsend, rrecv,
):
    me = lax.axis_index(AXIS)
    count = lax.axis_size(AXIS)
    right = lax.rem(me + 1, count)
    left = lax.rem(me + count - 1, count)

    smalls = [
        pltpu.make_async_copy(a, b, small_sem.at[i])
        for i, (a, b) in enumerate((
            (off_in, offs), (bases_in, bases_ref), (targ_in, targ_ref),
            (stiff_in, stiff_ref), (act_in, act_ref),
        ))
    ]
    for copy in smalls:
        copy.start()
    loads = {}
    for p in (0, 3, 1, 2):
        loads[p] = []
        for b in range(LB):
            lanes = pl.ds(b * 128, 128)
            for j, (rows, to) in enumerate((
                (pl.ds(0, NY), pl.ds(8, NY)),
                (pl.ds(NY - 8, 8), pl.ds(0, 8)),
                (pl.ds(0, 8), pl.ds(NY + 8, 8)),
            )):
                loads[p].append(pltpu.make_async_copy(
                    vel.at[:, p, rows, lanes], first.at[:, p, b, to, :], in_sem.at[p, b, j]
                ))
                loads[p][-1].start()

    barrier = pltpu.get_barrier_semaphore()
    for neighbour in (left, right):
        pl.semaphore_signal(barrier, inc=1, device_id=(neighbour,), device_id_type=MESH)

    for copy in smalls:
        copy.wait()
    lane = lax.broadcasted_iota(jnp.int32, (1, M), 1)
    living = jnp.where(lane < act_ref[...] * BLK, 1.0, 0.0)
    pack[0:3, :] = offs[...]
    pack[3:6, :] = targ_ref[...]
    pack[6:7, :] = living * stiff_ref[...]
    pack[7:8, :] = living
    pack[8:10, :] = bases_ref[0:2, :].astype(F32)
    pack[10:11, :] = (bases_ref[2:3, :] - me * CZ).astype(F32)
    pack[11:16, :] = jnp.zeros((5, M), F32)

    def prepare():
        o = marks[0:3, :]
        w = weights(o)
        force = marks[6:7, :] * (marks[3:6, :] - o)
        for j in range(4):
            taps[j : j + 1, :] = w[j][0:1]
            taps[4 + j : 5 + j, :] = w[j][1:2]
        for z in range(CZ):
            row = pick(z - cells[2:3, :], [w[j][2:3] for j in range(4)])
            zrows[z, 0:1, :] = row
            gains[z, 0:3, :] = force * row

    def tables():
        def xrow(i, _):
            r = pl.multiple_of(i * 16, 16)
            for half in (slice(0, M), slice(M, 2 * M)):
                where = lax.broadcasted_iota(jnp.int32, (16, M), 0) + r
                delta = (where - cells[0:1, half]) & (NX - 1)
                xtab[pl.ds(r, 16), half] = pick(delta, [taps[j : j + 1, half] for j in range(4)]).astype(BF)
            return 0

        lax.fori_loop(0, NX // 16, xrow, 0)

        def yrow(i, _):
            r = pl.multiple_of(i * 16, 16)
            for half in (slice(0, M), slice(M, 2 * M)):
                where = lax.broadcasted_iota(jnp.int32, (16, M), 0) + r
                delta = (where - cells[1:2, half]) & (NY - 1)
                ytab[pl.ds(r, 16), half] = pick(delta, [taps[4 + j : 5 + j, half] for j in range(4)])
            return 0

        lax.fori_loop(0, NY // 16, yrow, 0)

    core = lax.rem(me, 2)
    partner = (me + 1 - 2 * core, lax.rem(me + count - 1 + 2 * core, count))
    plane = (3 - 3 * core, 3 * core)
    inside = (2 - core, 1 + core)
    side = 1.0 - 2.0 * core.astype(F32)
    sides = (side, -side)

    lane128 = lax.broadcasted_iota(jnp.int32, (16, 128), 1)


    def stencil(p0, planes, src, put, near_planes, sign=None):
        per = NY // 64

        def rows(i, _):
            p = p0 + i // per
            base = pl.multiple_of((i % per) * 64, 64)
            for h in range(64 // 16):
                r = base + 16 * h
                turned = []
                for c in range(3):
                    v = [src[c, p, b, pl.ds(r + 8, 16), :] for b in range(LB)]
                    up = [pltpu.roll(x, 127, 1) for x in v]
                    down = [pltpu.roll(x, 1, 1) for x in v]
                    turned.append((
                        [jnp.where(lane128 == 127, up[(b + 1) % LB], up[b]) for b in range(LB)],
                        [jnp.where(lane128 == 0, down[(b - 1) % LB], down[b]) for b in range(LB)],
                    ))
                for b in range(LB):
                    v = [src[c, p, b, pl.ds(r + 8, 16), :] for c in range(3)]
                    upper, lower = [], []
                    for d in (2, 1, 0):
                        scaled = (0.5 * DT) * v[d]
                        if d == 2 and sign is not None:
                            scaled = sign * scaled
                        upper.append(DT * NU - scaled)
                        lower.append(DT * NU + scaled)
                    for c in range(3):
                        above, below = near_planes(c, p, b, r)
                        total = (1.0 - 6.0 * DT * NU) * v[c]
                        total = total + (upper[0] * above + lower[0] * below)
                        total = total + (
                            upper[1] * src[c, p, b, pl.ds(r + 9, 16), :]
                            + lower[1] * src[c, p, b, pl.ds(r + 7, 16), :]
                        )
                        total = total + (upper[2] * turned[c][0][b] + lower[2] * turned[c][1][b])
                        put(c, p, b, r, total)
            return 0

        lax.fori_loop(0, per * planes, rows, 0)

    def putter(step):
        def to_second(c, p, b, r, total):
            second[c, p, b, pl.ds(r + 8, 16), :] = total

        def to_output(c, p, b, r, total):
            vout[c, p, pl.ds(r, 16), b * 128 : b * 128 + 128] = total

        return to_second if step == 0 else to_output

    source = (first, second)

    def interior(step):
        src = source[step]
        stencil(
            1, 2, src, putter(step),
            lambda c, p, b, r: (
                src[c, p + 1, b, pl.ds(r + 8, 16), :], src[c, p - 1, b, pl.ds(r + 8, 16), :]
            ),
        )

    def border(k, step):
        src = source[step]
        stencil(
            plane[k], 1, src, putter(step),
            lambda c, p, b, r: (
                halo[step, k, c, pl.ds(r, 16), b * 128 : b * 128 + 128].astype(F32),
                src[c, inside[k], b, pl.ds(r + 8, 16), :],
            ),
            sides[k],
        )

    def spread(z, step):
        for c in range(3):
            lhs[c * NY : (c + 1) * NY, :] = (gains[z, c : c + 1, :] * ytab[...]).astype(BF)
        out = lax.dot_general(
            lhs[...], xtab[...], (((1,), (1,)), ((), ())), preferred_element_type=F32
        ).reshape(3, NY, NX)
        for b in range(LB):
            lanes = slice(b * 128, b * 128 + 128)
            if step == 0:
                total = second[:, z, b, 8 : NY + 8, :] + DT * out[:, :, lanes]
                second[:, z, b, 8 : NY + 8, :] = total
                second[:, z, b, 0:8, :] = total[:, NY - 8 :]
                second[:, z, b, NY + 8 :, :] = total[:, :8]
            else:
                total = vout[:, z, :, lanes] + DT * out[:, :, lanes]
                vout[:, z, :, lanes] = total
            low[z, :, :, lanes] = total.astype(BF)

    def sample(z):
        out = jnp.dot(low[z].reshape(3 * NY, NX), xtab[...], preferred_element_type=F32)
        y = ytab[...]
        parts = [jnp.sum(out[c * NY : (c + 1) * NY] * y, axis=0, keepdims=True) for c in range(3)]
        return jnp.concatenate(parts, axis=0) * zrows[z, 0:1, :]

    def sending(step, k, ref):
        return pltpu.make_async_remote_copy(
            src_ref=ref, dst_ref=halo.at[step, k],
            send_sem=send_sem.at[step, k], recv_sem=recv_sem.at[step, k],
            device_id=(partner[k],), device_id_type=MESH,
        )

    packet = pltpu.make_async_remote_copy(
        src_ref=pack, dst_ref=near, send_sem=psend, recv_sem=precv,
        device_id=(right,), device_id_type=MESH,
    )
    for c in loads[0] + loads[3]:
        c.wait()
    copies = [sending(0, k, edge.at[k]) for k in range(2)]
    for k in (1, 0):

        def lower_rows(i, _, k=k):
            r = pl.multiple_of(i * 16, 16)
            for c in range(3):
                for b in range(LB):
                    edge[k, c, pl.ds(r, 16), b * 128 : b * 128 + 128] = (
                        first[c, plane[k], b, pl.ds(r + 8, 16), :].astype(BF)
                    )
            return 0

        lax.fori_loop(0, NY // 16, lower_rows, 0)
        if k == 1:
            pl.semaphore_wait(barrier, 2)
            packet.start()
    copies[1].start()
    copies[0].start()
    for c in loads[1] + loads[2]:
        c.wait()
    interior(0)
    packet.wait_recv()
    marks[:, 0:M] = pack[...]
    marks[:, M:] = near[...]
    cells[0:2, :] = marks[8:10, :].astype(jnp.int32)
    cells[2:3, 0:M] = pack[10:11, :].astype(jnp.int32)
    cells[2:3, M:] = near[10:11, :].astype(jnp.int32) - CZ

    waits = [packet]
    for step in range(STEPS):
        last = step + 1 == STEPS
        prepare()
        tables()
        copies[0].wait()
        border(0, step)
        after = [] if last else [sending(step + 1, k, low.at[plane[k]]) for k in range(2)]

        def spread_one(i, _):
            spread(jnp.where(i == 2, plane[0], i + 1), step)
            return 0

        def sample_one(i, acc):
            return acc + sample(jnp.where(i == 2, plane[0], i + 1))

        lax.fori_loop(0, 3, spread_one, 0)
        if not last:
            after[0].start()
        acc = lax.fori_loop(0, 3, sample_one, jnp.zeros((3, 2 * M), F32))
        copies[1].wait()
        border(1, step)
        spread(plane[1], step)
        acc = acc + sample(plane[1])
        part[step, 0, 0:3, :] = acc[:, :M]
        part[step, 1, 0:3, :] = acc[:, M:]
        answers = [
            pltpu.make_async_remote_copy(
                src_ref=part.at[step, k], dst_ref=got.at[step, k],
                send_sem=rsend.at[step, k], recv_sem=rrecv.at[step, k],
                device_id=(target,), device_id_type=MESH,
            )
            for k, target in ((1, left), (0, right))[: 1 if last else 2]
        ]
        for c in answers:
            c.start()
        if not last:
            after[1].start()
            copies = after
            interior(step + 1)
        for c in answers:
            c.wait_recv()
        if last:
            oout[...] = marks[0:3, 0:M] + DT * (marks[7:8, 0:M] * (acc[:, :M] + got[step, 1, 0:3, :]))
        else:
            marks[0:3, 0:M] = marks[0:3, 0:M] + DT * (
                marks[7:8, 0:M] * (part[step, 0, 0:3, :] + got[step, 1, 0:3, :])
            )
            marks[0:3, M:] = marks[0:3, M:] + DT * (
                marks[7:8, M:] * (got[step, 0, 0:3, :] + part[step, 1, 0:3, :])
            )
        waits += answers
    for c in waits:
        c.wait_send()


def local(velocity, offsets, bases, targets, stiffness, active_block_count):
    vmem = pl.BlockSpec(memory_space=pltpu.VMEM)
    hbm = pl.BlockSpec(memory_space=pltpu.HBM)
    return pl.pallas_call(
        kernel,
        out_shape=(
            jax.ShapeDtypeStruct(velocity.shape, F32),
            jax.ShapeDtypeStruct(offsets.shape, F32),
        ),
        in_specs=[hbm] * 6,
        out_specs=(vmem, vmem),
        scratch_shapes=[
            pltpu.VMEM((3, CZ, LB, NY + 16, 128), F32),
            pltpu.VMEM((3, CZ, LB, NY + 16, 128), F32),
            pltpu.VMEM((CZ, 3, NY, NX), BF),
            pltpu.VMEM((2, 3, NY, NX), BF),
            pltpu.VMEM((STEPS, 2, 3, NY, NX), BF),
            pltpu.VMEM((NX, 2 * M), BF),
            pltpu.VMEM((NY, 2 * M), F32),
            pltpu.VMEM((3 * NY, 2 * M), BF),
            pltpu.VMEM((CZ, 8, 2 * M), F32),
            pltpu.VMEM((CZ, 8, 2 * M), F32),
            pltpu.VMEM((8, 2 * M), F32),
            pltpu.VMEM((8, 2 * M), jnp.int32),
            pltpu.VMEM((16, 2 * M), F32),
            pltpu.VMEM((16, M), F32),
            pltpu.VMEM((16, M), F32),
            pltpu.VMEM((STEPS, 2, 8, M), F32),
            pltpu.VMEM((STEPS, 2, 8, M), F32),
            pltpu.VMEM((3, M), F32),
            pltpu.VMEM((3, M), jnp.int32),
            pltpu.VMEM((3, M), F32),
            pltpu.VMEM((1, M), F32),
            pltpu.VMEM((1, 1), jnp.int32),
            pltpu.SemaphoreType.DMA((CZ, LB, 3)),
            pltpu.SemaphoreType.DMA((5,)),
            pltpu.SemaphoreType.DMA((STEPS, 2)),
            pltpu.SemaphoreType.DMA((STEPS, 2)),
            pltpu.SemaphoreType.DMA,
            pltpu.SemaphoreType.DMA,
            pltpu.SemaphoreType.DMA((STEPS, 2)),
            pltpu.SemaphoreType.DMA((STEPS, 2)),
        ],
        compiler_params=pltpu.CompilerParams(
            collective_id=0, has_side_effects=True, vmem_limit_bytes=40 * 1024 * 1024
        ),
    )(*(
        pltpu.with_memory_space_constraint(a, pltpu.HBM)
        for a in (
            velocity,
            offsets,
            bases,
            targets,
            stiffness.reshape(1, -1),
        )
    ), active_block_count.reshape(1, 1))


def solution(mesh):
    return jax.shard_map(
        local,
        mesh=mesh,
        in_specs=(
            P(None, AXIS, None, None),
            P(None, AXIS),
            P(None, AXIS),
            P(None, AXIS),
            P(AXIS),
            P(AXIS),
        ),
        out_specs=(P(None, AXIS, None, None), P(None, AXIS)),
        check_vma=False,
    )
```

time: 58.1 us -> 48.9 us (0.84)
  Pallas kernels: 53.4 us -> 44.1 us
    pallas_call x1, Pallas kernels: 53.4 us -> 44.1 us  [local(): pl.pallas_call(kernel, out_shape=(jax.ShapeDtypeStruct(velocity.shape, F3...]
where the time goes in v2:
time: 48.9 us; the launch traced here: 48.7 us
  Pallas kernels  44.1 us (90%)
  local copies, waits for them, and re-layouts  3.3 us (7%)
  between operations  1.29 us (3%)
    pallas_call x1, Pallas kernels, local(): pl.pallas_call(kernel, out_shape=(jax.ShapeDtypeStruct(velocity.shape, F3...  44.1 us
    unnamed x2, local copies, waits for them, and re-layouts  3.3 us

profile of v2, /device:TPU:0, one launch (start us, length us, event | category | flops | bytes accessed | tf_op | source)
XLA Modules:
  0.0 48.7 jit_solution(15215223041107178540)
XLA Ops:
  1.3 44.1 %shard_map.77 = (f32[3,4,256,512]{3,2,1,0:T(8,128)S(1)}, f32[3,512]{1,0:T(4,128)S(1)}) custom-call(f32[3,4,256,512]{3,2,1,0:T(8,128)} %vel.1, f32[3,512]{1,0:T(4,128)} %off_in.1, s32[3,512]{1,0:T(4,128)} %bases_in.1, f32[3,512]{1,0:T(4,128)} %targ_in.1, f32[1,512]{1,0:T(1,128)} %bitcast.3, s32[1,1]{1,0:T(1,128)} %bitcast.2.act_in), custom_call_target="tpu_custom_call" | custom-call | tf_op jit(solution)/shard_map/pallas_call | solution.py:329
  45.4 2.7 %copy.11 = f32[3,4,256,512]{3,2,1,0:T(8,128)} copy(f32[3,4,256,512]{3,2,1,0:T(8,128)S(1)} %get-tuple-element.4) | data formatting | bytes 12582912
  48.1 0.6 %copy.12 = f32[3,512]{1,0:T(4,128)} copy(f32[3,512]{1,0:T(4,128)S(1)} %get-tuple-element.5) | data formatting | bytes 12288

commit v3 on v2

v3 whole, which is shorter than its diff:
```python
import math

import jax
import jax.numpy as jnp
from jax import lax
from jax.experimental import pallas as pl
from jax.experimental.pallas import tpu as pltpu
from jax.sharding import PartitionSpec as P

AXIS = "gz"
BLK = 256
STEPS = 2
DT = 0.2
NU = 0.3
CZ = 4
NY = 256
NX = 512
M = 512
LB = NX // 128
MESH = pl.DeviceIdType.MESH
BF = jnp.bfloat16
F32 = jnp.float32


def weights(offsets):
    angle = offsets * (0.5 * math.pi)
    c = 0.25 * jnp.cos(angle)
    s = 0.25 * jnp.sin(angle)
    return (0.25 + c, 0.25 + s, 0.25 - c, 0.25 - s)


def pick(delta, taps):
    out = jnp.where(delta == 3, taps[3], 0.0)
    for j in (2, 1, 0):
        out = jnp.where(delta == j, taps[j], out)
    return out


def kernel(
    vel, off_in, bases_in, targ_in, stiff_in, act_in,
    vout, oout,
    inner_a, outer_a, inner_b, outer_b, low, edge, halo, xtab, ytab, lhs, gains, zrows, taps, cells, marks, pack, near,
    sums, part, got, offs, bases_ref, targ_ref, stiff_ref, act_ref,
    in_sem, small_sem, send_sem, recv_sem, psend, precv, rsend, rrecv,
):
    me = lax.axis_index(AXIS)
    count = lax.axis_size(AXIS)
    right = lax.rem(me + 1, count)
    left = lax.rem(me + count - 1, count)

    smalls = [
        pltpu.make_async_copy(a, b, small_sem.at[i])
        for i, (a, b) in enumerate((
            (off_in, offs), (bases_in, bases_ref), (targ_in, targ_ref),
            (stiff_in, stiff_ref), (act_in, act_ref),
        ))
    ]
    for copy in smalls:
        copy.start()
    sets = ((inner_a, outer_a), (inner_b, outer_b))
    loads = {}
    for p in (0, 3, 1, 2):
        home, at = (outer_a, p // 3) if p in (0, 3) else (inner_a, p - 1)
        loads[p] = []
        for b in range(LB):
            lanes = pl.ds(b * 128, 128)
            for j, (rows, to) in enumerate((
                (pl.ds(0, NY), pl.ds(8, NY)),
                (pl.ds(NY - 8, 8), pl.ds(0, 8)),
                (pl.ds(0, 8), pl.ds(NY + 8, 8)),
            )):
                loads[p].append(pltpu.make_async_copy(
                    vel.at[:, p, rows, lanes], home.at[:, at, b, to, :], in_sem.at[p, b, j]
                ))
                loads[p][-1].start()

    barrier = pltpu.get_barrier_semaphore()
    for neighbour in (left, right):
        pl.semaphore_signal(barrier, inc=1, device_id=(neighbour,), device_id_type=MESH)

    for copy in smalls:
        copy.wait()
    lane = lax.broadcasted_iota(jnp.int32, (1, M), 1)
    living = jnp.where(lane < act_ref[...] * BLK, 1.0, 0.0)
    pack[0:3, :] = offs[...]
    pack[3:6, :] = targ_ref[...]
    pack[6:7, :] = living * stiff_ref[...]
    pack[7:8, :] = living
    pack[8:10, :] = bases_ref[0:2, :].astype(F32)
    pack[10:11, :] = (bases_ref[2:3, :] - me * CZ).astype(F32)
    pack[11:16, :] = jnp.zeros((5, M), F32)

    def prepare(half):
        o = marks[0:3, half]
        w = weights(o)
        force = marks[6:7, half] * (marks[3:6, half] - o)
        for j in range(4):
            taps[j : j + 1, half] = w[j][0:1]
            taps[4 + j : 5 + j, half] = w[j][1:2]
        for z in range(CZ):
            row = pick(z - cells[8:9, half], [w[j][2:3] for j in range(4)])
            zrows[z, 0:1, half] = row
            gains[z, 0:3, half] = force * row

    def tables(halves):
        def fill(table, extent, first, kind):
            def rows(i, _):
                r = pl.multiple_of(i * 32, 32)
                for half in halves:
                    where = lax.broadcasted_iota(jnp.int32, (32, M), 0) + r
                    out = 0.0
                    for j in range(4):
                        out = jnp.where(
                            where == cells[first + j : first + j + 1, half],
                            taps[first + j : first + j + 1, half],
                            out,
                        )
                    table[pl.ds(r, 32), half] = out.astype(kind)
                return 0

            lax.fori_loop(0, extent // 32, rows, 0)

        fill(xtab, NX, 0, BF)
        fill(ytab, NY, 4, F32)

    core = lax.rem(me, 2)
    partner = (me + 1 - 2 * core, lax.rem(me + count - 1 + 2 * core, count))
    plane = (3 - 3 * core, 3 * core)
    at = (1 - core, core)
    side = 1.0 - 2.0 * core.astype(F32)
    sides = (side, -side)
    lane128 = lax.broadcasted_iota(jnp.int32, (16, 128), 1)

    def stencil(src, dst, p, base, height, near_planes, sign=None):
        for h in range(height // 16):
            r = base + 16 * h
            turned = []
            for c in range(3):
                v = [src[c, p, b, pl.ds(r + 8, 16), :] for b in range(LB)]
                up = [pltpu.roll(x, 127, 1) for x in v]
                down = [pltpu.roll(x, 1, 1) for x in v]
                turned.append((
                    [jnp.where(lane128 == 127, up[(b + 1) % LB], up[b]) for b in range(LB)],
                    [jnp.where(lane128 == 0, down[(b - 1) % LB], down[b]) for b in range(LB)],
                ))
            for b in range(LB):
                v = [src[c, p, b, pl.ds(r + 8, 16), :] for c in range(3)]
                upper, lower = [], []
                for d in (2, 1, 0):
                    scaled = (0.5 * DT) * v[d]
                    if d == 2 and sign is not None:
                        scaled = sign * scaled
                    upper.append(DT * NU - scaled)
                    lower.append(DT * NU + scaled)
                for c in range(3):
                    above, below = near_planes(c, b, r)
                    total = (1.0 - 6.0 * DT * NU) * v[c]
                    total = total + (upper[0] * above + lower[0] * below)
                    total = total + (
                        upper[1] * src[c, p, b, pl.ds(r + 9, 16), :]
                        + lower[1] * src[c, p, b, pl.ds(r + 7, 16), :]
                    )
                    total = total + (upper[2] * turned[c][0][b] + lower[2] * turned[c][1][b])
                    dst[c, p, b, pl.ds(r + 8, 16), :] = total

    def interior(step):
        (inn, out), (dst, _) = sets[step], sets[1 - step]
        for q in (0, 1):

            def near_planes(c, b, r, q=q):
                middle = inn[c, 1 - q, b, pl.ds(r + 8, 16), :]
                edge_plane = out[c, q, b, pl.ds(r + 8, 16), :]
                return (edge_plane, middle) if q else (middle, edge_plane)

            def rows(i, _, q=q, near_planes=near_planes):
                stencil(inn, dst, q, pl.multiple_of(i * 128, 128), 128, near_planes)
                return 0

            lax.fori_loop(0, NY // 128, rows, 0)

    def border(k, step, start, stop):
        (inn, out), (_, dst) = sets[step], sets[1 - step]

        def near_planes(c, b, r):
            return (
                halo[step, k, c, pl.ds(r, 16), b * 128 : b * 128 + 128].astype(F32),
                inn[c, at[k], b, pl.ds(r + 8, 16), :],
            )

        def rows(i, _):
            stencil(out, dst, at[k], pl.multiple_of(i * 128, 128), 128, near_planes, sides[k])
            return 0

        lax.fori_loop(start // 128, stop // 128, rows, 0)

    def spread(z, kind, q, step, start=0, stop=NY, width=2 * M):
        work = sets[1 - step][kind]
        height = stop - start
        for c in range(3):
            lhs[c * height : (c + 1) * height, 0:width] = (
                gains[z, c : c + 1, 0:width] * ytab[start:stop, 0:width]
            ).astype(BF)
        out = lax.dot_general(
            lhs[0 : 3 * height, 0:width],
            xtab[:, 0:width],
            (((1,), (1,)), ((), ())),
            preferred_element_type=F32,
        ).reshape(3, height, NX)
        for b in range(LB):
            lanes = slice(b * 128, b * 128 + 128)
            total = work[:, q, b, start + 8 : stop + 8, :] + DT * out[:, :, lanes]
            if step + 1 < STEPS:
                work[:, q, b, start + 8 : stop + 8, :] = total
                if stop == NY:
                    work[:, q, b, 0:8, :] = total[:, height - 8 :]
                if start == 0:
                    work[:, q, b, NY + 8 :, :] = total[:, :8]
            else:
                vout[:, z, start:stop, lanes] = total
            low[z, :, start:stop, lanes] = total.astype(BF)

    own, other = slice(0, M), slice(M, 2 * M)
    both = slice(0, 2 * M)

    def reduce_rows(out, z, half):
        y = ytab[:, half]
        parts = [jnp.sum(out[c * NY : (c + 1) * NY] * y, axis=0, keepdims=True) for c in range(3)]
        return jnp.concatenate(parts, axis=0) * zrows[z, 0:1, half]

    def sample(z, half=both):
        out = jnp.dot(low[z].reshape(3 * NY, NX), xtab[:, half], preferred_element_type=F32)
        return reduce_rows(out, z, half)

    def spread_outer(k, step, start, stop):
        @pl.when(core == k)
        def _():
            spread(CZ - 1, 1, 1, step, start, stop, M)

        @pl.when(core != k)
        def _():
            spread(0, 1, 0, step, start, stop)

    def sample_outer(k):
        @pl.when(core == k)
        def _():
            sums[0:3, own] = sums[0:3, own] + sample(CZ - 1, own)

        @pl.when(core != k)
        def _():
            sums[0:3, :] = sums[0:3, :] + sample(0)

    def sample_planes(planes, half):
        total = 0.0
        for z in range(planes):
            out = jnp.dot(low[z].reshape(3 * NY, NX), xtab[:, half], preferred_element_type=F32)
            total = total + reduce_rows(out, z, half)
        return total

    pieces = ((0, 0, NY), (1, 0, NY // 2), (1, NY // 2, NY))

    def sending(step, ref_of):
        out = []
        for i, (k, start, stop) in enumerate(pieces):
            rows = pl.ds(start, stop - start)
            out.append(pltpu.make_async_remote_copy(
                src_ref=ref_of(k).at[:, rows, :], dst_ref=halo.at[step, k, :, rows, :],
                send_sem=send_sem.at[step, i], recv_sem=recv_sem.at[step, i],
                device_id=(partner[k],), device_id_type=MESH,
            ))
        return out

    packet = pltpu.make_async_remote_copy(
        src_ref=pack, dst_ref=near, send_sem=psend, recv_sem=precv,
        device_id=(right,), device_id_type=MESH,
    )
    for c in loads[0] + loads[3]:
        c.wait()
    copies = sending(0, lambda k: edge.at[k])
    for k in (1, 0):

        def lower_rows(i, _, k=k):
            r = pl.multiple_of(i * 16, 16)
            for c in range(3):
                for b in range(LB):
                    edge[k, c, pl.ds(r, 16), b * 128 : b * 128 + 128] = (
                        outer_a[c, at[k], b, pl.ds(r + 8, 16), :].astype(BF)
                    )
            return 0

        lax.fori_loop(0, NY // 16, lower_rows, 0)
    pl.semaphore_wait(barrier, 2)
    packet.start()
    for i in (1, 0, 2):
        copies[i].start()
    for c in loads[1] + loads[2]:
        c.wait()
    interior(0)
    marks[:, own] = pack[...]

    def columns(half, shift):
        for j in range(4):
            cells[j : j + 1, half] = (marks[8:9, half].astype(jnp.int32) + j) & (NX - 1)
            cells[4 + j : 5 + j, half] = (marks[9:10, half].astype(jnp.int32) + j) & (NY - 1)
        cells[8:9, half] = marks[10:11, half].astype(jnp.int32) - shift

    waits = [packet]
    for step in range(STEPS):
        last = step + 1 == STEPS
        if step == 0:
            columns(own, 0)
            prepare(own)
            tables((own,))
            packet.wait_recv()
            marks[:, other] = near[...]
            columns(other, CZ)
            prepare(other)
            tables((other,))
        else:
            prepare(both)
            tables((own, other))
        copies[0].wait()
        border(0, step, 0, NY)
        after = [] if last else sending(step + 1, lambda k: low.at[plane[k]])

        def spread_one(i, _):
            spread(1 + i, 0, i, step)
            return 0

        def sample_one(i, acc):
            return acc + sample(1 + i)

        lax.fori_loop(0, 2, spread_one, 0)
        spread_outer(0, step, 0, NY)
        if not last:
            after[0].start()
        copies[1].wait()
        border(1, step, 0, NY // 2)
        spread_outer(1, step, 0, NY // 2)
        if not last:
            after[1].start()
            sums[0:3, :] = lax.fori_loop(0, 2, sample_one, jnp.zeros((3, 2 * M), F32))
            sample_outer(0)
        copies[2].wait()
        border(1, step, NY // 2, NY)
        spread_outer(1, step, NY // 2, NY)
        if last:
            part[step, 1, 0:3, :] = sample_planes(CZ - 1, other)
        else:
            sample_outer(1)
            part[step, 0, 0:3, :] = sums[0:3, own]
            part[step, 1, 0:3, :] = sums[0:3, other]
        answers = [
            pltpu.make_async_remote_copy(
                src_ref=part.at[step, k], dst_ref=got.at[step, k],
                send_sem=rsend.at[step, k], recv_sem=rrecv.at[step, k],
                device_id=(target,), device_id_type=MESH,
            )
            for k, target in ((1, left), (0, right))[: 1 if last else 2]
        ]
        for c in answers:
            c.start()
        if last:
            acc = sample_planes(CZ, own)
        else:
            after[2].start()
            copies = after
            interior(step + 1)
        for c in answers:
            c.wait_recv()
        if last:
            oout[...] = marks[0:3, own] + DT * (marks[7:8, own] * (acc + got[step, 1, 0:3, :]))
        else:
            marks[0:3, own] = marks[0:3, own] + DT * (
                marks[7:8, own] * (part[step, 0, 0:3, :] + got[step, 1, 0:3, :])
            )
            marks[0:3, other] = marks[0:3, other] + DT * (
                marks[7:8, other] * (got[step, 0, 0:3, :] + part[step, 1, 0:3, :])
            )
        waits += answers
    for c in waits:
        c.wait_send()


def local(velocity, offsets, bases, targets, stiffness, active_block_count):
    vmem = pl.BlockSpec(memory_space=pltpu.VMEM)
    hbm = pl.BlockSpec(memory_space=pltpu.HBM)
    return pl.pallas_call(
        kernel,
        out_shape=(
            jax.ShapeDtypeStruct(velocity.shape, F32),
            jax.ShapeDtypeStruct(offsets.shape, F32),
        ),
        in_specs=[hbm] * 6,
        out_specs=(vmem, vmem),
        scratch_shapes=[
            pltpu.VMEM((3, 2, LB, NY + 16, 128), F32),
            pltpu.VMEM((3, 2, LB, NY + 16, 128), F32),
            pltpu.VMEM((3, 2, LB, NY + 16, 128), F32),
            pltpu.VMEM((3, 2, LB, NY + 16, 128), F32),
            pltpu.VMEM((CZ, 3, NY, NX), BF),
            pltpu.VMEM((2, 3, NY, NX), BF),
            pltpu.VMEM((STEPS, 2, 3, NY, NX), BF),
            pltpu.VMEM((NX, 2 * M), BF),
            pltpu.VMEM((NY, 2 * M), F32),
            pltpu.VMEM((3 * NY, 2 * M), BF),
            pltpu.VMEM((CZ, 8, 2 * M), F32),
            pltpu.VMEM((CZ, 8, 2 * M), F32),
            pltpu.VMEM((8, 2 * M), F32),
            pltpu.VMEM((16, 2 * M), jnp.int32),
            pltpu.VMEM((16, 2 * M), F32),
            pltpu.VMEM((16, M), F32),
            pltpu.VMEM((16, M), F32),
            pltpu.VMEM((8, 2 * M), F32),
            pltpu.VMEM((STEPS, 2, 8, M), F32),
            pltpu.VMEM((STEPS, 2, 8, M), F32),
            pltpu.VMEM((3, M), F32),
            pltpu.VMEM((3, M), jnp.int32),
            pltpu.VMEM((3, M), F32),
            pltpu.VMEM((1, M), F32),
            pltpu.VMEM((1, 1), jnp.int32),
            pltpu.SemaphoreType.DMA((CZ, LB, 3)),
            pltpu.SemaphoreType.DMA((5,)),
            pltpu.SemaphoreType.DMA((STEPS, 3)),
            pltpu.SemaphoreType.DMA((STEPS, 3)),
            pltpu.SemaphoreType.DMA,
            pltpu.SemaphoreType.DMA,
            pltpu.SemaphoreType.DMA((STEPS, 2)),
            pltpu.SemaphoreType.DMA((STEPS, 2)),
        ],
        compiler_params=pltpu.CompilerParams(
            collective_id=0, has_side_effects=True, vmem_limit_bytes=40 * 1024 * 1024
        ),
    )(*(
        pltpu.with_memory_space_constraint(a, pltpu.HBM)
        for a in (
            velocity,
            offsets,
            bases,
            targets,
            stiffness.reshape(1, -1),
        )
    ), active_block_count.reshape(1, 1))


def solution(mesh):
    return jax.shard_map(
        local,
        mesh=mesh,
        in_specs=(
            P(None, AXIS, None, None),
            P(None, AXIS),
            P(None, AXIS),
            P(None, AXIS),
            P(AXIS),
            P(AXIS),
        ),
        out_specs=(P(None, AXIS, None, None), P(None, AXIS)),
        check_vma=False,
    )
```

time: 48.9 us -> 44.5 us (0.910)
  Pallas kernels: 44.1 us -> 39.8 us
    pallas_call x1, Pallas kernels: 44.1 us -> 39.8 us  [local(): pl.pallas_call(kernel, out_shape=(jax.ShapeDtypeStruct(velocity.shape, F3...]
where the time goes in v3:
time: 44.5 us; the launch traced here: 44.4 us
  Pallas kernels  39.8 us (89%)
  local copies, waits for them, and re-layouts  3.3 us (7%)
  between operations  1.29 us (3%)
    pallas_call x1, Pallas kernels, local(): pl.pallas_call(kernel, out_shape=(jax.ShapeDtypeStruct(velocity.shape, F3...  39.8 us
    unnamed x2, local copies, waits for them, and re-layouts  3.3 us

profile of v3, /device:TPU:0, one launch (start us, length us, event | category | flops | bytes accessed | tf_op | source)
XLA Modules:
  0.0 44.4 jit_solution(7903838245289350902)
XLA Ops:
  1.3 39.8 %shard_map.77 = (f32[3,4,256,512]{3,2,1,0:T(8,128)S(1)}, f32[3,512]{1,0:T(4,128)S(1)}) custom-call(f32[3,4,256,512]{3,2,1,0:T(8,128)} %vel.1, f32[3,512]{1,0:T(4,128)} %off_in.1, s32[3,512]{1,0:T(4,128)} %bases_in.1, f32[3,512]{1,0:T(4,128)} %targ_in.1, f32[1,512]{1,0:T(1,128)} %bitcast.3, s32[1,1]{1,0:T(1,128)} %bitcast.2.act_in), custom_call_target="tpu_custom_call" | custom-call | tf_op jit(solution)/shard_map/pallas_call | solution.py:387
  41.1 2.7 %copy.11 = f32[3,4,256,512]{3,2,1,0:T(8,128)} copy(f32[3,4,256,512]{3,2,1,0:T(8,128)S(1)} %get-tuple-element.4) | data formatting | bytes 12582912
  43.8 0.6 %copy.12 = f32[3,512]{1,0:T(4,128)} copy(f32[3,512]{1,0:T(4,128)S(1)} %get-tuple-element.5) | data formatting | bytes 12288

commit v4 on v3

--- a/solution.py
+++ b/solution.py
@@ -48,6 +48,10 @@
     right = lax.rem(me + 1, count)
     left = lax.rem(me + count - 1, count)
 
+    core = lax.rem(me, 2)
+    partner = (me + 1 - 2 * core, lax.rem(me + count - 1 + 2 * core, count))
+    plane = (3 - 3 * core, 3 * core)
+    at = (1 - core, core)
     smalls = [
         pltpu.make_async_copy(a, b, small_sem.at[i])
         for i, (a, b) in enumerate((
@@ -59,9 +63,14 @@
         copy.start()
     sets = ((inner_a, outer_a), (inner_b, outer_b))
     loads = {}
-    for p in (0, 3, 1, 2):
-        home, at = (outer_a, p // 3) if p in (0, 3) else (inner_a, p - 1)
-        loads[p] = []
+    for key, p, home, q in (
+        ("slow", plane[1], outer_a, at[1]),
+        ("fast", plane[0], outer_a, at[0]),
+        (1, 1, inner_a, 0),
+        (2, 2, inner_a, 1),
+    ):
+        number = len(loads)
+        loads[key] = []
         for b in range(LB):
             lanes = pl.ds(b * 128, 128)
             for j, (rows, to) in enumerate((
@@ -69,10 +78,10 @@
                 (pl.ds(NY - 8, 8), pl.ds(0, 8)),
                 (pl.ds(0, 8), pl.ds(NY + 8, 8)),
             )):
-                loads[p].append(pltpu.make_async_copy(
-                    vel.at[:, p, rows, lanes], home.at[:, at, b, to, :], in_sem.at[p, b, j]
+                loads[key].append(pltpu.make_async_copy(
+                    vel.at[:, p, rows, lanes], home.at[:, q, b, to, :], in_sem.at[number, b, j]
                 ))
-                loads[p][-1].start()
+                loads[key][-1].start()
 
     barrier = pltpu.get_barrier_semaphore()
     for neighbour in (left, right):
@@ -123,10 +132,6 @@
         fill(xtab, NX, 0, BF)
         fill(ytab, NY, 4, F32)
 
-    core = lax.rem(me, 2)
-    partner = (me + 1 - 2 * core, lax.rem(me + count - 1 + 2 * core, count))
-    plane = (3 - 3 * core, 3 * core)
-    at = (1 - core, core)
     side = 1.0 - 2.0 * core.astype(F32)
     sides = (side, -side)
     lane128 = lax.broadcasted_iota(jnp.int32, (16, 128), 1)
@@ -147,9 +152,8 @@
                 v = [src[c, p, b, pl.ds(r + 8, 16), :] for c in range(3)]
                 upper, lower = [], []
                 for d in (2, 1, 0):
-                    scaled = (0.5 * DT) * v[d]
-                    if d == 2 and sign is not None:
-                        scaled = sign * scaled
+                    rate = 0.5 * DT if d != 2 or sign is None else 0.5 * DT * sign
+                    scaled = rate * v[d]
                     upper.append(DT * NU - scaled)
                     lower.append(DT * NU + scaled)
                 for c in range(3):
@@ -163,9 +167,9 @@
                     total = total + (upper[2] * turned[c][0][b] + lower[2] * turned[c][1][b])
                     dst[c, p, b, pl.ds(r + 8, 16), :] = total
 
-    def interior(step):
+    def interior(step, which=(0, 1)):
         (inn, out), (dst, _) = sets[step], sets[1 - step]
-        for q in (0, 1):
+        for q in which:
 
             def near_planes(c, b, r, q=q):
                 middle = inn[c, 1 - q, b, pl.ds(r + 8, 16), :]
@@ -178,17 +182,17 @@
 
             lax.fori_loop(0, NY // 128, rows, 0)
 
-    def border(k, step, start, stop):
+    def border(slot, q, sign, step, start, stop):
         (inn, out), (_, dst) = sets[step], sets[1 - step]
 
         def near_planes(c, b, r):
             return (
-                halo[step, k, c, pl.ds(r, 16), b * 128 : b * 128 + 128].astype(F32),
-                inn[c, at[k], b, pl.ds(r + 8, 16), :],
+                halo[step, slot, c, pl.ds(r, 16), b * 128 : b * 128 + 128].astype(F32),
+                inn[c, q, b, pl.ds(r + 8, 16), :],
             )
 
         def rows(i, _):
-            stencil(out, dst, at[k], pl.multiple_of(i * 128, 128), 128, near_planes, sides[k])
+            stencil(out, dst, q, pl.multiple_of(i * 128, 128), 128, near_planes, sign)
             return 0
 
         lax.fori_loop(start // 128, stop // 128, rows, 0)
@@ -250,10 +254,12 @@
             sums[0:3, :] = sums[0:3, :] + sample(0)
 
     def sample_planes(planes, half):
+        out = jnp.dot(
+            low[0:planes].reshape(planes * 3 * NY, NX), xtab[:, half], preferred_element_type=F32
+        )
         total = 0.0
         for z in range(planes):
-            out = jnp.dot(low[z].reshape(3 * NY, NX), xtab[:, half], preferred_element_type=F32)
-            total = total + reduce_rows(out, z, half)
+            total = total + reduce_rows(out[z * 3 * NY : (z + 1) * 3 * NY], z, half)
         return total
 
     pieces = ((0, 0, NY), (1, 0, NY // 2), (1, NY // 2, NY))
@@ -273,12 +279,10 @@
         src_ref=pack, dst_ref=near, send_sem=psend, recv_sem=precv,
         device_id=(right,), device_id_type=MESH,
     )
-    for c in loads[0] + loads[3]:
-        c.wait()
     copies = sending(0, lambda k: edge.at[k])
-    for k in (1, 0):
-
-        def lower_rows(i, _, k=k):
+
+    def lower_edge(k):
+        def rows(i, _):
             r = pl.multiple_of(i * 16, 16)
             for c in range(3):
                 for b in range(LB):
@@ -287,15 +291,7 @@
                     )
             return 0
 
-        lax.fori_loop(0, NY // 16, lower_rows, 0)
-    pl.semaphore_wait(barrier, 2)
-    packet.start()
-    for i in (1, 0, 2):
-        copies[i].start()
-    for c in loads[1] + loads[2]:
-        c.wait()
-    interior(0)
-    marks[:, own] = pack[...]
+        lax.fori_loop(0, NY // 16, rows, 0)
 
     def columns(half, shift):
         for j in range(4):
@@ -303,81 +299,91 @@
             cells[4 + j : 5 + j, half] = (marks[9:10, half].astype(jnp.int32) + j) & (NY - 1)
         cells[8:9, half] = marks[10:11, half].astype(jnp.int32) - shift
 
-    waits = [packet]
-    for step in range(STEPS):
-        last = step + 1 == STEPS
-        if step == 0:
-            columns(own, 0)
-            prepare(own)
-            tables((own,))
-            packet.wait_recv()
-            marks[:, other] = near[...]
-            columns(other, CZ)
-            prepare(other)
-            tables((other,))
-        else:
-            prepare(both)
-            tables((own, other))
-        copies[0].wait()
-        border(0, step, 0, NY)
-        after = [] if last else sending(step + 1, lambda k: low.at[plane[k]])
-
-        def spread_one(i, _):
-            spread(1 + i, 0, i, step)
-            return 0
-
-        def sample_one(i, acc):
-            return acc + sample(1 + i)
-
-        lax.fori_loop(0, 2, spread_one, 0)
-        spread_outer(0, step, 0, NY)
-        if not last:
-            after[0].start()
-        copies[1].wait()
-        border(1, step, 0, NY // 2)
-        spread_outer(1, step, 0, NY // 2)
-        if not last:
-            after[1].start()
-            sums[0:3, :] = lax.fori_loop(0, 2, sample_one, jnp.zeros((3, 2 * M), F32))
-            sample_outer(0)
-        copies[2].wait()
-        border(1, step, NY // 2, NY)
-        spread_outer(1, step, NY // 2, NY)
-        if last:
-            part[step, 1, 0:3, :] = sample_planes(CZ - 1, other)
-        else:
-            sample_outer(1)
-            part[step, 0, 0:3, :] = sums[0:3, own]
-            part[step, 1, 0:3, :] = sums[0:3, other]
-        answers = [
-            pltpu.make_async_remote_copy(
-                src_ref=part.at[step, k], dst_ref=got.at[step, k],
-                send_sem=rsend.at[step, k], recv_sem=rrecv.at[step, k],
-                device_id=(target,), device_id_type=MESH,
-            )
-            for k, target in ((1, left), (0, right))[: 1 if last else 2]
-        ]
-        for c in answers:
-            c.start()
-        if last:
-            acc = sample_planes(CZ, own)
-        else:
-            after[2].start()
-            copies = after
-            interior(step + 1)
-        for c in answers:
-            c.wait_recv()
-        if last:
-            oout[...] = marks[0:3, own] + DT * (marks[7:8, own] * (acc + got[step, 1, 0:3, :]))
-        else:
-            marks[0:3, own] = marks[0:3, own] + DT * (
-                marks[7:8, own] * (part[step, 0, 0:3, :] + got[step, 1, 0:3, :])
-            )
-            marks[0:3, other] = marks[0:3, other] + DT * (
-                marks[7:8, other] * (got[step, 0, 0:3, :] + part[step, 1, 0:3, :])
-            )
-        waits += answers
-    for c in waits:
+    for c in loads["slow"]:
+        c.wait()
+    lower_edge(1)
+    pl.semaphore_wait(barrier, 2)
+    packet.start()
+    copies[1].start()
+    copies[2].start()
+    for c in loads["fast"]:
+        c.wait()
+    lower_edge(0)
+    copies[0].start()
+    marks[:, own] = pack[...]
+    columns(own, 0)
+    prepare(own)
+    tables((own,))
+    for c in loads[1] + loads[2]:
+        c.wait()
+    interior(0)
+    def outer_border(k, step, start, stop):
+        border(k, at[k], sides[k], step, start, stop)
+
+    copies[0].wait()
+    outer_border(0, 0, 0, NY)
+    packet.wait_recv()
+    marks[:, other] = near[...]
+    columns(other, CZ)
+    prepare(other)
+    tables((other,))
+
+    spread(1, 0, 0, 0)
+    spread(2, 0, 1, 0)
+    spread_outer(0, 0, 0, NY)
+    after = sending(1, lambda k: low.at[plane[k]])
+    after[0].start()
+    copies[1].wait()
+    outer_border(1, 0, 0, NY // 2)
+    spread_outer(1, 0, 0, NY // 2)
+    after[1].start()
+    sums[0:3, :] = sample(1) + sample(2)
+    sample_outer(0)
+    copies[2].wait()
+    outer_border(1, 0, NY // 2, NY)
+    spread_outer(1, 0, NY // 2, NY)
+    sample_outer(1)
+    part[0, 0, 0:3, :] = sums[0:3, own]
+    part[0, 1, 0:3, :] = sums[0:3, other]
+
+    def exchange(step, k, target):
+        return pltpu.make_async_remote_copy(
+            src_ref=part.at[step, k], dst_ref=got.at[step, k],
+            send_sem=rsend.at[step, k], recv_sem=rrecv.at[step, k],
+            device_id=(target,), device_id_type=MESH,
+        )
+
+    answers = [exchange(0, 0, right), exchange(0, 1, left)]
+    for c in answers:
+        c.start()
+    after[2].start()
+    interior(1)
+    after[0].wait()
+    outer_border(0, 1, 0, NY)
+    for c in answers:
+        c.wait_recv()
+    marks[0:3, own] = marks[0:3, own] + DT * (
+        marks[7:8, own] * (part[0, 0, 0:3, :] + got[0, 1, 0:3, :])
+    )
+    marks[0:3, other] = marks[0:3, other] + DT * (
+        marks[7:8, other] * (got[0, 0, 0:3, :] + part[0, 1, 0:3, :])
+    )
+    prepare(both)
+    tables((own, other))
+    spread(1, 0, 0, 1)
+    spread(2, 0, 1, 1)
+    for c in after[1:]:
+        c.wait()
+    outer_border(1, 1, 0, NY)
+    spread(0, 1, 0, 1)
+    part[1, 1, 0:3, :] = sample_planes(CZ - 1, other)
+    answer = exchange(1, 1, left)
+    answer.start()
+    spread(CZ - 1, 1, 1, 1, 0, NY, M)
+    acc = sample_planes(CZ, own)
+    answer.wait_recv()
+    oout[...] = marks[0:3, own] + DT * (marks[7:8, own] * (acc + got[1, 1, 0:3, :]))
+    for c in [packet, answer] + answers:
         c.wait_send()
 
 

time: 44.5 us -> 43.9 us (0.987)
  Pallas kernels: 39.8 us -> 39.1 us
    pallas_call x1, Pallas kernels: 39.8 us -> 39.1 us  [local(): pl.pallas_call(kernel, out_shape=(jax.ShapeDtypeStruct(velocity.shape, F3...]
where the time goes in v4:
time: 43.9 us; the launch traced here: 43.7 us
  Pallas kernels  39.1 us (89%)
  local copies, waits for them, and re-layouts  3.3 us (8%)
  between operations  1.29 us (3%)
    pallas_call x1, Pallas kernels, local(): pl.pallas_call(kernel, out_shape=(jax.ShapeDtypeStruct(velocity.shape, F3...  39.1 us
    unnamed x2, local copies, waits for them, and re-layouts  3.3 us

profile of v4, /device:TPU:0, one launch (start us, length us, event | category | flops | bytes accessed | tf_op | source)
XLA Modules:
  0.0 43.7 jit_solution(8934285472253919950)
XLA Ops:
  1.3 39.1 %shard_map.77 = (f32[3,4,256,512]{3,2,1,0:T(8,128)S(1)}, f32[3,512]{1,0:T(4,128)S(1)}) custom-call(f32[3,4,256,512]{3,2,1,0:T(8,128)} %vel.1, f32[3,512]{1,0:T(4,128)} %off_in.1, s32[3,512]{1,0:T(4,128)} %bases_in.1, f32[3,512]{1,0:T(4,128)} %targ_in.1, f32[1,512]{1,0:T(1,128)} %bitcast.3, s32[1,1]{1,0:T(1,128)} %bitcast.2.act_in), custom_call_target="tpu_custom_call" | custom-call | tf_op jit(solution)/shard_map/pallas_call | solution.py:393
  40.4 2.7 %copy.11 = f32[3,4,256,512]{3,2,1,0:T(8,128)} copy(f32[3,4,256,512]{3,2,1,0:T(8,128)S(1)} %get-tuple-element.4) | data formatting | bytes 12582912
  43.1 0.6 %copy.12 = f32[3,512]{1,0:T(4,128)} copy(f32[3,512]{1,0:T(4,128)S(1)} %get-tuple-element.5) | data formatting | bytes 12288

commit v5 on v4

--- a/solution.py
+++ b/solution.py
@@ -177,10 +177,10 @@
                 return (edge_plane, middle) if q else (middle, edge_plane)
 
             def rows(i, _, q=q, near_planes=near_planes):
-                stencil(inn, dst, q, pl.multiple_of(i * 128, 128), 128, near_planes)
+                stencil(inn, dst, q, pl.multiple_of(i * 256, 256), 256, near_planes)
                 return 0
 
-            lax.fori_loop(0, NY // 128, rows, 0)
+            lax.fori_loop(0, NY // 256, rows, 0)
 
     def border(slot, q, sign, step, start, stop):
         (inn, out), (_, dst) = sets[step], sets[1 - step]

time: 43.9 us -> 43.9 us (level)
  no operation moved by 1% of the time
where the time goes in v5:
time: 43.9 us; the launch traced here: 43.7 us
  Pallas kernels  39.1 us (89%)
  local copies, waits for them, and re-layouts  3.3 us (8%)
  between operations  1.29 us (3%)
    pallas_call x1, Pallas kernels, local(): pl.pallas_call(kernel, out_shape=(jax.ShapeDtypeStruct(velocity.shape, F3...  39.1 us
    unnamed x2, local copies, waits for them, and re-layouts  3.3 us

profile of v5, /device:TPU:0, one launch (start us, length us, event | category | flops | bytes accessed | tf_op | source)
XLA Modules:
  0.0 43.7 jit_solution(12167659365932280407)
XLA Ops:
  1.3 39.1 %shard_map.77 = (f32[3,4,256,512]{3,2,1,0:T(8,128)S(1)}, f32[3,512]{1,0:T(4,128)S(1)}) custom-call(f32[3,4,256,512]{3,2,1,0:T(8,128)} %vel.1, f32[3,512]{1,0:T(4,128)} %off_in.1, s32[3,512]{1,0:T(4,128)} %bases_in.1, f32[3,512]{1,0:T(4,128)} %targ_in.1, f32[1,512]{1,0:T(1,128)} %bitcast.3, s32[1,1]{1,0:T(1,128)} %bitcast.2.act_in), custom_call_target="tpu_custom_call" | custom-call | tf_op jit(solution)/shard_map/pallas_call | solution.py:393
  40.4 2.7 %copy.11 = f32[3,4,256,512]{3,2,1,0:T(8,128)} copy(f32[3,4,256,512]{3,2,1,0:T(8,128)S(1)} %get-tuple-element.4) | data formatting | bytes 12582912
  43.1 0.6 %copy.12 = f32[3,512]{1,0:T(4,128)} copy(f32[3,512]{1,0:T(4,128)S(1)} %get-tuple-element.5) | data formatting | bytes 12288
